TPU v7x, 32 devices: a whole 2x2x4 slice. The times are simulated.
32 devices in a mesh: graphs: 2 (over y), rows: 4 (over z), cols: 2 (over x), sub: 2 (over core).
Axes of the slice: x: 2, y: 2, z: 4, core: 2. Of those that a mesh axis runs over, the one named last changes fastest.
Arguments:
- current_block: float32 [16, 65536], P(None, ('graphs', 'rows', 'cols', 'sub')), parts along dimension 1, may hold values from -1200 to 1200, as said below
- previous_block: float32 [16, 65536], P(None, ('graphs', 'rows', 'cols', 'sub')), parts along dimension 1, may hold values from -1200 to 1200, as said below
- adjacency_tiles: float32 [1536, 128, 128], P(('graphs', 'rows', 'cols', 'sub')), parts along dimension 0, may hold values from -0.3125 to 0.3125
- tile_rows: int32 [1536], P(('graphs', 'rows', 'cols', 'sub')), parts along dimension 0, may hold values from 0 to 255, as said below
- tile_cols: int32 [1536], P(('graphs', 'rows', 'cols', 'sub')), parts along dimension 0, may hold values from 0 to 255, as said below
- tile_count: int32 [32], P(('graphs', 'rows', 'cols', 'sub')), parts along dimension 0, may hold values from 18 to 48, as said below
- locked: int32 [2], P('graphs'), parts along dimension 0, may hold values from 0 to 7
Outputs:
- w_basis: float32 [16, 65536], P(None, ('graphs', 'rows', 'cols', 'sub')), parts along dimension 1
- w_image: float32 [16, 65536], P(None, ('graphs', 'rows', 'cols', 'sub')), parts along dimension 1
- ritz_matrix: float32 [96, 48], P('graphs'), parts along dimension 0
There are 2 independent parts, one for each index of `graphs`. A program takes and returns all parts, laid end to end along the dimension named above; each array names one. Nothing has to cross between parts.
Inputs may be any that keep to these rules, and one draw needn't show every extreme that they name: `current_block`: entries of order one to some hundreds. `previous_block`: entries of order one to some hundreds. Slots d * 48 to (d + 1) * 48 - 1 belong to device d and name its own tile rows d * 16 to (d + 1) * 16 - 1. The first 16 slots of a device name its tile rows in order, with tile_cols equal to tile_rows. Slots past the device's count name tile row d * 16 and carry no weight. `tile_cols`: A slot of device d names a tile column from d * 16 - 8 to (d + 1) * 16 + 7. Slot 16 of a device names a tile of the block before it and slot 17 one of the block after it, where such a block exists. A pair of tile row and tile column may stand in several slots; their tiles add. `tile_count`: in every draw some device has all 48 slots live.
All inputs are finite; a program needn't handle non-finite values.
Results may differ from a plain program's by a relative error of at most 0.000094.
Values sent between devices are 32-bit elements; how exact they have to be, the bound alone decides.
A program may use at most 64 MiB of HBM per device.

v0:
```python
import functools

import jax
import jax.numpy as jnp
from jax import lax
from jax.experimental import pallas as pl
from jax.experimental.pallas import tpu as pltpu
from jax.sharding import PartitionSpec as P

MESH = pl.DeviceIdType.MESH
F32 = jnp.float32
BF16 = jnp.bfloat16
HIGHEST = lax.Precision.HIGHEST
NT_DIMS = (((1,), (1,)), ((), ()))


def split(values):
    high = values.astype(BF16)
    return high, (values - high.astype(F32)).astype(BF16)


def iota(shape, dim):
    return lax.broadcasted_iota(jnp.int32, shape, dim)


def gather_kernel(
    sizes,
    cols_ref, rows_ref, count_ref, locked_ref, x_hbm, p_hbm, tiles_ref,
    r_hbm, ar_hbm, early_ref, late_ref,
    x_ref, p_ref, r_ref, ar_ref, raw, halves, xh, ph, yh, q_buf, z_buf, extra, mine_q, all_q,
    mine_e, near_e, line_e, far_e, mine_g, near_g, line_g, far_g, block_sem, out_sem, tile_sem, halo_send, halo_recv, near_send, near_recv, far_send, far_recv, all_send, all_recv,
):
    row_count, col_count, sub_count = sizes
    near_count = col_count * sub_count
    vectors, here = x_ref.shape
    slots, tile, _ = tiles_ref.shape
    row_tiles = here // tile
    reach = row_tiles // 2
    spare = slots - row_tiles
    chunk = row_tiles // 2
    chunks = slots // chunk

    row_at = lax.axis_index("rows")
    near_at = lax.axis_index("cols") * sub_count + lax.axis_index("sub")
    position = row_at * near_count + near_at
    total = row_count * near_count

    def place(spot):
        return {
            "rows": spot // near_count,
            "cols": (spot % near_count) // sub_count,
            "sub": spot % sub_count,
        }

    def near_device(index):
        return {"cols": index // sub_count, "sub": index % sub_count}

    def far_device(index):
        return {"rows": index}

    block_copies = (
        pltpu.make_async_copy(x_hbm, x_ref, block_sem.at[0]),
        pltpu.make_async_copy(p_hbm, p_ref, block_sem.at[1]),
    )
    for copy in block_copies:
        copy.start()
    tile_copies = []
    for c in range(chunks):
        part = pl.ds(c * chunk, chunk)
        tile_copies.append(pltpu.make_async_copy(tiles_ref.at[part], raw.at[part], tile_sem.at[c]))
        tile_copies[-1].start()

    has_left = position > 0
    has_right = position < total - 1
    barrier = pltpu.get_barrier_semaphore()

    for k in range(1, total):
        pl.semaphore_signal(
            barrier, inc=1, device_id=place((position + k) % total), device_id_type=MESH
        )
    for copy in block_copies:
        copy.wait()
    for t in range(row_tiles):
        xh[reach + t] = x_ref[:, t * tile : (t + 1) * tile]
        ph[reach + t] = p_ref[:, t * tile : (t + 1) * tile]
    pl.semaphore_wait(barrier, total - 1)

    def halo_copies(buffer, which):
        left = pltpu.make_async_remote_copy(
            src_ref=buffer.at[pl.ds(reach, reach)],
            dst_ref=buffer.at[pl.ds(reach + row_tiles, reach)],
            send_sem=halo_send.at[which, 0],
            recv_sem=halo_recv.at[which, 0],
            device_id=place(position - 1),
            device_id_type=MESH,
        )
        right = pltpu.make_async_remote_copy(
            src_ref=buffer.at[pl.ds(row_tiles, reach)],
            dst_ref=buffer.at[pl.ds(0, reach)],
            send_sem=halo_send.at[which, 1],
            recv_sem=halo_recv.at[which, 1],
            device_id=place(position + 1),
            device_id_type=MESH,
        )
        return left, right

    def halo_start(copies):
        left, right = copies

        @pl.when(has_left)
        def _():
            left.start()

        @pl.when(has_right)
        def _():
            right.start()

    def halo_arrived(copies):
        left, right = copies

        @pl.when(has_right)
        def _():
            left.wait_recv()

        @pl.when(has_left)
        def _():
            right.wait_recv()

    def halo_sent(copies):
        left, right = copies

        @pl.when(has_left)
        def _():
            left.wait_send()

        @pl.when(has_right)
        def _():
            right.wait_send()

    x_halo = halo_copies(xh, 0)
    p_halo = halo_copies(ph, 1)
    y_halo = halo_copies(yh, 2)
    halo_start(x_halo)
    halo_start(p_halo)

    def product(block, slot):
        high, low = split(block)
        lhs = jnp.concatenate(
            [jnp.concatenate([high, high], axis=1), jnp.concatenate([low, low], axis=1)], axis=0
        )
        out = jnp.dot(lhs, halves[slot], preferred_element_type=F32)
        return out[:vectors] + out[vectors:]

    def flat(buffer, start):
        return jnp.concatenate([buffer[start + t] for t in range(row_tiles)], axis=1)

    def split_tiles(c):
        tile_copies[c].wait()

        def step(i, carry):
            t = c * chunk + i
            high, low = split(raw[t])
            halves[t, 0:tile, :] = high
            halves[t, tile : 2 * tile, :] = low
            return carry

        lax.fori_loop(0, chunk, step, 0)

    def diagonal(source, target, target_base):
        def step(g, carry):
            for i in range(8):
                r = g * 8 + i
                target[target_base + r] = product(source[reach + r], r)
            return carry

        lax.fori_loop(0, row_tiles // 8, step, 0)

    live = count_ref[0]
    base_col = position * row_tiles - reach
    base_row = position * row_tiles
    places = [
        jnp.where(row_tiles + t < live, rows_ref[row_tiles + t] - base_row, -1) for t in range(spare)
    ]

    def scattered(padded, target, target_base):
        for t in range(spare):
            index = jnp.clip(cols_ref[row_tiles + t] - base_col, 0, 2 * row_tiles - 1)
            extra[t] = product(padded[index], row_tiles + t)

        def gather(g, carry):
            some = [g * 4 + i for i in range(4)]
            sums = [target[target_base + r] for r in some]
            for t in range(spare):
                block = extra[t]
                for i, r in enumerate(some):
                    sums[i] = sums[i] + block * jnp.where(places[t] == r, 1.0, 0.0).astype(F32)
            for i, r in enumerate(some):
                target[target_base + r] = sums[i]
            return carry

        lax.fori_loop(0, row_tiles // 4, gather, 0)

    def exchange(mine, buffer, count, at, device, send, recv, which):
        copies = []
        for k in range(1, count):
            other = (at + k) % count
            copies.append(
                (
                    pltpu.make_async_remote_copy(
                        src_ref=mine,
                        dst_ref=buffer.at[at],
                        send_sem=send.at[which, k],
                        recv_sem=recv.at[which, at],
                        device_id=device(other),
                        device_id_type=MESH,
                    ),
                    pltpu.make_async_remote_copy(
                        src_ref=mine,
                        dst_ref=buffer.at[other],
                        send_sem=send.at[which, k],
                        recv_sem=recv.at[which, other],
                        device_id=device(other),
                        device_id_type=MESH,
                    ),
                )
            )
        for out, _ in copies:
            out.start()
        buffer[at] = mine[...]
        return copies

    def collect(copies, buffer, count):
        for _, arriving in copies:
            arriving.wait_recv()
        out = buffer[0]
        for k in range(1, count):
            out = out + buffer[k]
        return out

    def flush(copies):
        for out, _ in copies:
            out.wait_send()

    for c in range(chunks):
        split_tiles(c)
        if c == row_tiles // chunk - 1:
            diagonal(xh, yh, reach)
    diagonal(ph, q_buf, 0)
    halo_arrived(x_halo)
    scattered(xh, yh, reach)
    halo_start(y_halo)

    x = x_ref[...]
    xx = jnp.sum(x * x, axis=1, keepdims=True)
    y = flat(yh, reach)
    xy = jnp.sum(x * y, axis=1, keepdims=True)
    lane = iota((vectors, 128), 1)
    line = iota((vectors, 128), 0)
    on_first = lane == line
    on_second = lane == line + vectors
    mine_q[...] = jnp.sum(
        jnp.where(on_first, xx, 0.0) + jnp.where(on_second, xy, 0.0), axis=0, keepdims=True
    )
    all_copies = exchange(mine_q, all_q, total, position, place, all_send, all_recv, 0)

    halo_arrived(p_halo)
    scattered(ph, q_buf, 0)
    p = p_ref[...]
    x_parts, y_parts, p_parts, q_parts = [split(v) for v in (x, y, p, flat(q_buf, 0))]
    gap = jnp.zeros((vectors, here), BF16)

    def inner(left, right):
        lhs = jnp.concatenate([v[0] for v in left] + [v[1] for v in left], axis=0)
        out = None
        for half in range(2):
            rhs = jnp.concatenate([gap if v is None else v[half] for v in right], axis=0)
            term = lax.dot_general(lhs, rhs, NT_DIMS, preferred_element_type=F32)
            out = term if out is None else out + term
        count = len(left) * vectors
        return out[:count] + out[count:]

    wide = 6 * vectors
    mine_e[...] = jnp.zeros_like(mine_e)
    mine_e[:, 0:wide] = inner(
        (x_parts, p_parts), (x_parts, None, p_parts, y_parts, None, q_parts)
    )
    near_e_copies = exchange(
        mine_e, near_e, near_count, near_at, near_device, near_send, near_recv, 1
    )

    diagonal(yh, z_buf, 0)
    halo_arrived(y_halo)
    scattered(yh, z_buf, 0)

    sums = jnp.broadcast_to(collect(all_copies, all_q, total), (vectors, 128))
    xx_all = jnp.sum(jnp.where(on_first, sums, 0.0), axis=1, keepdims=True)
    xy_all = jnp.sum(jnp.where(on_second, sums, 0.0), axis=1, keepdims=True)
    shift = (xy_all + 1e-06) / (xx_all + 1e-06)
    free = iota((vectors, 1), 0) >= locked_ref[0]
    residual = jnp.where(free, shift * x - y, 0.0)
    carried = jnp.where(free, shift * y - flat(z_buf, 0), 0.0)
    r_ref[...] = residual
    ar_ref[...] = residual - carried
    outs = (
        pltpu.make_async_copy(r_ref, r_hbm, out_sem.at[0]),
        pltpu.make_async_copy(ar_ref, ar_hbm, out_sem.at[1]),
    )
    for copy in outs:
        copy.start()
    r_parts, n_parts = split(residual), split(carried)
    plain = inner((r_parts,), (x_parts, r_parts, p_parts, y_parts, n_parts, q_parts))
    other = inner((n_parts,), (x_parts, r_parts, p_parts, x_parts, r_parts, p_parts))
    first_half = iota((vectors, wide), 1) < 3 * vectors
    mine_g[...] = jnp.zeros_like(mine_g)
    mine_g[:, 0:wide] = jnp.where(first_half, plain, 0.5 * (plain + other))
    near_g_copies = exchange(
        mine_g, near_g, near_count, near_at, near_device, near_send, near_recv, 2
    )
    line_e[...] = collect(near_e_copies, near_e, near_count)
    far_e_copies = exchange(line_e, far_e, row_count, row_at, far_device, far_send, far_recv, 1)
    line_g[...] = collect(near_g_copies, near_g, near_count)
    far_g_copies = exchange(line_g, far_g, row_count, row_at, far_device, far_send, far_recv, 2)
    early_ref[...] = collect(far_e_copies, far_e, row_count)
    late_ref[...] = collect(far_g_copies, far_g, row_count)

    for copy in outs:
        copy.wait()
    halo_sent(x_halo)
    halo_sent(p_halo)
    halo_sent(y_halo)
    flush(all_copies)
    flush(near_e_copies)
    flush(far_e_copies)
    flush(near_g_copies)
    flush(far_g_copies)


def finish_kernel(
    vertex_total, locked_ref, r_hbm, ar_hbm, early_ref, late_ref, w_hbm, aw_hbm, ritz_ref,
    upper, r_buf, ar_buf, w_buf, aw_buf, in_sem, out_sem,
):
    vectors = r_buf.shape[0]
    width = 3 * vectors
    ins = (
        pltpu.make_async_copy(r_hbm, r_buf, in_sem.at[0]),
        pltpu.make_async_copy(ar_hbm, ar_buf, in_sem.at[1]),
    )
    outs = (
        pltpu.make_async_copy(w_buf, w_hbm, out_sem.at[0]),
        pltpu.make_async_copy(aw_buf, aw_hbm, out_sem.at[1]),
    )
    for copy in ins:
        copy.start()
    scale = 1.0 / vertex_total
    early = early_ref[...] * scale
    late = late_ref[...] * scale
    locked = locked_ref[0]

    lane_w = iota((vectors, 128), 1)
    line_w = iota((vectors, 128), 0)
    frozen = (lane_w == line_w + vectors) & (line_w < locked)
    small = late + jnp.where(frozen, 1.0, 0.0)
    small = jnp.where((lane_w >= vectors) & (lane_w < 2 * vectors), small, 0.0)
    small = small + jnp.where(lane_w == line_w + 2 * vectors, 1.0, 0.0)

    lane = iota((width, 128), 1)
    line = iota((width, 128), 0)
    outer = (line < vectors) | (line >= 2 * vectors)
    pick = jnp.concatenate(
        [
            jnp.where(outer & (lane == line), 1.0, 0.0),
            jnp.where(outer & (lane == line + width), 1.0, 0.0),
        ],
        axis=1,
    )
    above = jnp.zeros((vectors, 128), F32)
    set_first = jnp.concatenate([above, late, above, above, above, above, above, above], axis=0)
    set_second = jnp.concatenate([above, above, above, above, late, above, above, above], axis=0)
    turned = lax.dot_general(
        pick, jnp.concatenate([set_first, set_second], axis=1), NT_DIMS,
        precision=HIGHEST, preferred_element_type=F32,
    )
    gram = jnp.concatenate([early[:vectors], late, early[vectors:]], axis=0) + turned
    padded = (line == lane) & (line >= vectors) & (line < vectors + locked)
    big = jnp.where(lane < width, gram + jnp.where(padded, 1.0, 0.0), 0.0)
    big = big + jnp.where(lane == line + width, 1.0, 0.0)

    def panel(matrix, k, shift, count):
        rows = [matrix[k + i : k + i + 1, :] for i in range(count)]
        columns = [
            jnp.broadcast_to(matrix[:, shift + k + i : shift + k + i + 1], matrix.shape)
            for i in range(count)
        ]
        block = {
            (i, j): jnp.broadcast_to(rows[i][:, shift + k + j : shift + k + j + 1], (1, 128))
            for i in range(count)
            for j in range(i, count)
        }
        done = []
        for m in range(count):
            inverse = 1.0 / block[m, m]
            done.append(rows[m] * lax.rsqrt(block[m, m]))
            factors = {j: block[m, j] * inverse for j in range(m + 1, count)}
            for i in range(m + 1, count):
                for j in range(i, count):
                    block[i, j] = block[i, j] - factors[i] * block[m, j]
                rows[i] = rows[i] - factors[i] * rows[m]
                columns[i] = columns[i] - factors[i] * columns[m]
            matrix = matrix - columns[m] * (rows[m] * inverse)
        return matrix, done

    for copy in ins:
        copy.wait()
    step = 4
    small_rows = []
    for k in range(0, vectors, step):
        small, done = panel(small, k, vectors, step)
        small_rows += done
    inverse_w = jnp.concatenate(small_rows, axis=0)[:, 2 * vectors : 3 * vectors]
    for k in range(0, width, step):
        if k == 2 * vectors:
            w_buf[...] = jnp.dot(
                inverse_w, r_buf[...], precision=HIGHEST, preferred_element_type=F32
            )
            aw_buf[...] = jnp.dot(
                inverse_w, ar_buf[...], precision=HIGHEST, preferred_element_type=F32
            )
            for copy in outs:
                copy.start()
        big, done = panel(big, k, 0, step)
        for i in range(step):
            upper[k + i : k + i + 1, :] = done[i]
    inverse = upper[:, width : 2 * width]
    image = gram[:, :width] - gram[:, width : 2 * width]
    half = jnp.dot(inverse, image, precision=HIGHEST, preferred_element_type=F32)
    first = lax.dot_general(half, inverse, NT_DIMS, precision=HIGHEST, preferred_element_type=F32)
    second = lax.dot_general(inverse, half, NT_DIMS, precision=HIGHEST, preferred_element_type=F32)
    ritz_ref[...] = 0.5 * (first + second)
    for copy in outs:
        copy.wait()


def body(sizes, current_block, previous_block, adjacency_tiles, tile_rows, tile_cols, tile_count, locked):
    vectors, here = current_block.shape
    slots, tile, _ = adjacency_tiles.shape
    row_tiles = here // tile
    row_count, col_count, sub_count = sizes
    near_count = col_count * sub_count
    chunks = slots // (row_tiles // 2)
    width = 3 * vectors
    smem = pl.BlockSpec(memory_space=pltpu.SMEM)
    vmem = pl.BlockSpec(memory_space=pltpu.VMEM)
    anywhere = pl.BlockSpec(memory_space=pl.ANY)
    dma = pltpu.SemaphoreType.DMA
    residual, residual_image, early, late = pl.pallas_call(
        functools.partial(gather_kernel, sizes),
        out_shape=(
            jax.ShapeDtypeStruct((vectors, here), F32),
            jax.ShapeDtypeStruct((vectors, here), F32),
            jax.ShapeDtypeStruct((2 * vectors, 128), F32),
            jax.ShapeDtypeStruct((vectors, 128), F32),
        ),
        in_specs=[smem] * 4 + [anywhere] * 3,
        out_specs=(anywhere, anywhere, vmem, vmem),
        scratch_shapes=[
            pltpu.VMEM((vectors, here), F32),
            pltpu.VMEM((vectors, here), F32),
            pltpu.VMEM((vectors, here), F32),
            pltpu.VMEM((vectors, here), F32),
            pltpu.VMEM((slots, tile, tile), F32),
            pltpu.VMEM((slots, 2 * tile, tile), BF16),
            pltpu.VMEM((2 * row_tiles, vectors, tile), F32),
            pltpu.VMEM((2 * row_tiles, vectors, tile), F32),
            pltpu.VMEM((2 * row_tiles, vectors, tile), F32),
            pltpu.VMEM((row_tiles, vectors, tile), F32),
            pltpu.VMEM((row_tiles, vectors, tile), F32),
            pltpu.VMEM((slots - row_tiles, vectors, tile), F32),
            pltpu.VMEM((1, 128), F32),
            pltpu.VMEM((row_count * near_count, 1, 128), F32),
            pltpu.VMEM((2 * vectors, 128), F32),
            pltpu.VMEM((near_count, 2 * vectors, 128), F32),
            pltpu.VMEM((2 * vectors, 128), F32),
            pltpu.VMEM((row_count, 2 * vectors, 128), F32),
            pltpu.VMEM((vectors, 128), F32),
            pltpu.VMEM((near_count, vectors, 128), F32),
            pltpu.VMEM((vectors, 128), F32),
            pltpu.VMEM((row_count, vectors, 128), F32),
            dma((2,)),
            dma((2,)),
            dma((chunks,)),
            dma((3, 2)),
            dma((3, 2)),
            dma((3, near_count)),
            dma((3, near_count)),
            dma((3, row_count)),
            dma((3, row_count)),
            dma((1, row_count * near_count)),
            dma((1, row_count * near_count)),
        ],
        compiler_params=pltpu.CompilerParams(collective_id=0, has_side_effects=True),
        name="operator_and_grams",
    )(tile_cols, tile_rows, tile_count, locked, current_block, previous_block, adjacency_tiles)
    vertex_total = here * row_count * near_count
    return pl.pallas_call(
        functools.partial(finish_kernel, vertex_total),
        out_shape=(
            jax.ShapeDtypeStruct((vectors, here), F32),
            jax.ShapeDtypeStruct((vectors, here), F32),
            jax.ShapeDtypeStruct((width, width), F32),
        ),
        in_specs=[smem] + [anywhere] * 2 + [vmem] * 2,
        out_specs=(anywhere, anywhere, vmem),
        scratch_shapes=[pltpu.VMEM((width, 128), F32)]
        + [pltpu.VMEM((vectors, here), F32)] * 4
        + [dma((2,)), dma((2,))],
        name="factor_and_project",
    )(locked, residual, residual_image, early, late)


def solution(mesh):
    split_all = ("graphs", "rows", "cols", "sub")
    sizes = tuple(mesh.shape[name] for name in ("rows", "cols", "sub"))
    in_specs = (
        P(None, split_all),
        P(None, split_all),
        P(split_all, None, None),
        P(split_all),
        P(split_all),
        P(split_all),
        P("graphs"),
    )
    out_specs = (P(None, split_all), P(None, split_all), P("graphs", None))
    return jax.shard_map(
        functools.partial(body, sizes), mesh=mesh, in_specs=in_specs, out_specs=out_specs, check_vma=False
    )
```

profile of v0, /device:TPU:0, one launch (start us, length us, event | category | flops | bytes accessed | tf_op | source)
XLA Modules:
  0.0 29.9 jit_solution(16316260470645366046)
XLA Ops:
  1.9 23.4 %operator_and_grams.1 = (f32[16,2048]{1,0:T(8,128)}, f32[16,2048]{1,0:T(8,128)}, f32[32,128]{1,0:T(8,128)}, f32[16,128]{1,0:T(8,128)}) custom-call(s32[48]{0:T(128)} %cols_ref.1, s32[48]{0:T(128)} %rows_ref.1, s32[1]{0:T(128)S(6)} %copy.10.count_ref, s32[1]{0:T(128)S(6)} %copy.11.locked_ref, f32[16,2048]{1,0:T(8,128)} %x_hbm.1, f32[16,2048]{1,0:T(8,128)} %p_hbm.1, ...), custom_call_target="tpu_custom_call" | custom-call | tf_op jit(solution)/shard_map/operator_and_grams/pallas_call | solution.py:455
  25.3 4.6 %factor_and_project.1 = (f32[16,2048]{1,0:T(8,128)}, f32[16,2048]{1,0:T(8,128)}, f32[48,48]{1,0:T(8,128)}) custom-call(s32[1]{0:T(128)S(6)} %copy.11.locked_ref, f32[16,2048]{1,0:T(8,128)} %get-tuple-element.7.r_hbm, f32[16,2048]{1,0:T(8,128)} %get-tuple-element.8.ar_hbm, f32[32,128]{1,0:T(8,128)} %get-tuple-element.9.early_ref, ...), custom_call_target="tpu_custom_call" | custom-call | tf_op jit(solution)/shard_map/factor_and_project/pallas_call | solution.py:504
where the time goes:
time: 30.2 us; the launch traced here: 29.9 us
  Pallas kernels  28 us (93%)
  between operations  1.93 us (6%)
    pallas_call x1, Pallas kernels, body(): pl.pallas_call(functools.partial(gather_kernel, sizes), out_shape=(jax.Sh...  23.4 us
    pallas_call x1, Pallas kernels, body(): pl.pallas_call(functools.partial(finish_kernel, vertex_total), out_shape=...  4.61 us

commit v1 on v0

v1 whole, which is shorter than its diff:
```python
import functools

import jax
import jax.numpy as jnp
from jax import lax
from jax.experimental import pallas as pl
from jax.experimental.pallas import tpu as pltpu
from jax.sharding import PartitionSpec as P

MESH = pl.DeviceIdType.MESH
F32 = jnp.float32
BF16 = jnp.bfloat16
HIGHEST = lax.Precision.HIGHEST
NT_DIMS = (((1,), (1,)), ((), ()))
EDGE = 8
VMEM_ALL = 67043328
VMEM_ROOM = 10600 * 1024


def split(values):
    high = values.astype(BF16)
    return high, (values - high.astype(F32)).astype(BF16)


def iota(shape, dim):
    return lax.broadcasted_iota(jnp.int32, shape, dim)


def tree_sum(terms):
    while len(terms) > 1:
        terms = [a + b for a, b in zip(terms[::2], terms[1::2])] + terms[len(terms) & ~1 :]
    return terms[0]


def panel(matrix, k, shift, count):
    rows = [matrix[k + i : k + i + 1, :] for i in range(count)]
    columns = [
        jnp.broadcast_to(matrix[:, shift + k + i : shift + k + i + 1], matrix.shape)
        for i in range(count)
    ]
    block = {
        (i, j): jnp.broadcast_to(rows[i][:, shift + k + j : shift + k + j + 1], (1, 128))
        for i in range(count)
        for j in range(i, count)
    }
    done = []
    for m in range(count):
        inverse = 1.0 / block[m, m]
        done.append(rows[m] * lax.rsqrt(block[m, m]))
        factors = {j: block[m, j] * inverse for j in range(m + 1, count)}
        for i in range(m + 1, count):
            for j in range(i, count):
                block[i, j] = block[i, j] - factors[i] * block[m, j]
            rows[i] = rows[i] - factors[i] * rows[m]
            columns[i] = columns[i] - factors[i] * columns[m]
        matrix = matrix - columns[m] * (rows[m] * inverse)
    return matrix, done


def iterate_kernel(
    sizes, vertex_total,
    cols_in, rows_in, count_in, locked_in, x_hbm, p_hbm, tiles_hbm,
    w_ref, aw_ref, ritz_ref,
    cols_ref, rows_ref, count_ref, locked_ref, index_ref, before_ref, last_ref,
    raw, halves, xh, ph, yh, q_buf, z_buf, seg, mine, every, upper,
    int_sem, block_sem, tile_sem, halo_send, halo_recv, all_send, all_recv,
):
    row_count, col_count, sub_count = sizes
    near_count = col_count * sub_count
    total = row_count * near_count
    vectors, here = w_ref.shape
    slots, tile, _ = raw.shape
    row_tiles = here // tile
    reach = row_tiles // 2
    spare = slots - row_tiles
    chunk = row_tiles
    chunks = slots // chunk
    width = 3 * vectors

    row_at = lax.axis_index("rows")
    col_at = lax.axis_index("cols")
    sub_at = lax.axis_index("sub")
    position = row_at * near_count + col_at * sub_count + sub_at

    def place(spot):
        return {
            "rows": lax.div(spot, near_count),
            "cols": lax.div(lax.rem(spot, near_count), sub_count),
            "sub": lax.rem(spot, sub_count),
        }

    rows_from = [lax.rem(row_at + k, row_count) for k in range(row_count)]
    cols_from = [lax.rem(col_at + k, col_count) for k in range(col_count)]
    subs_from = [lax.rem(sub_at + k, sub_count) for k in range(sub_count)]

    def each_peer(act):
        if total <= 32:
            for k in range(1, total):
                act(
                    {
                        "rows": rows_from[k // near_count],
                        "cols": cols_from[k % near_count // sub_count],
                        "sub": subs_from[k % sub_count],
                    }
                )
        else:

            def step(k, carry):
                act(place(lax.rem(position + k, total)))
                return carry

            lax.fori_loop(1, total, step, 0)

    barrier = pltpu.get_barrier_semaphore()
    each_peer(
        lambda device: pl.semaphore_signal(barrier, inc=1, device_id=device, device_id_type=MESH)
    )

    own = pl.ds(reach, row_tiles)

    def block_start(source, target, sem):
        for t in range(row_tiles):
            pltpu.make_async_copy(
                source.at[:, pl.ds(t * tile, tile)], target.at[reach + t], sem
            ).start()

    def block_wait(target, sem):
        pltpu.make_async_copy(target.at[own], target.at[own], sem).wait()

    block_start(x_hbm, xh, block_sem.at[0])
    int_copies = [
        pltpu.make_async_copy(source, target, int_sem.at[i])
        for i, (source, target) in enumerate(
            (
                (cols_in, cols_ref),
                (rows_in, rows_ref),
                (count_in, count_ref),
                (locked_in, locked_ref),
            )
        )
    ]
    for copy in int_copies:
        copy.start()
    tile_copies = []
    for c in range(chunks):
        part = pl.ds(c * chunk, chunk)
        tile_copies.append(pltpu.make_async_copy(tiles_hbm.at[part], raw.at[part], tile_sem.at[c]))
    tile_copies[0].start()
    block_start(p_hbm, ph, block_sem.at[1])
    for copy in tile_copies[1:]:
        copy.start()

    has_left = position > 0
    has_right = position < total - 1
    left_device = place(lax.max(position - 1, 0))
    right_device = place(lax.min(position + 1, total - 1))

    def halo_copies(buffer, which):
        left = pltpu.make_async_remote_copy(
            src_ref=buffer.at[pl.ds(reach, reach)],
            dst_ref=buffer.at[pl.ds(reach + row_tiles, reach)],
            send_sem=halo_send.at[which, 0],
            recv_sem=halo_recv.at[which, 0],
            device_id=left_device,
            device_id_type=MESH,
        )
        right = pltpu.make_async_remote_copy(
            src_ref=buffer.at[pl.ds(row_tiles, reach)],
            dst_ref=buffer.at[pl.ds(0, reach)],
            send_sem=halo_send.at[which, 1],
            recv_sem=halo_recv.at[which, 1],
            device_id=right_device,
            device_id_type=MESH,
        )
        return left, right

    def halo_do(first_when, first, second_when, second):
        @pl.when(first_when)
        def _():
            first()

        @pl.when(second_when)
        def _():
            second()

    def halo_start(copies):
        halo_do(has_left, copies[0].start, has_right, copies[1].start)

    def halo_arrived(copies):
        halo_do(has_right, copies[0].wait_recv, has_left, copies[1].wait_recv)

    def halo_sent(copies):
        halo_do(has_left, copies[0].wait_send, has_right, copies[1].wait_send)

    x_halo = halo_copies(xh, 0)
    p_halo = halo_copies(ph, 1)
    y_halo = halo_copies(yh, 2)

    block_wait(xh, block_sem.at[0])
    pl.semaphore_wait(barrier, total - 1)
    halo_start(x_halo)
    block_wait(ph, block_sem.at[1])
    halo_start(p_halo)

    def product(block, slot):
        high, low = split(block)
        lhs = jnp.concatenate(
            [jnp.concatenate([high, high], axis=1), jnp.concatenate([low, low], axis=1)], axis=0
        )
        out = jnp.dot(lhs, halves[slot], preferred_element_type=F32)
        return out[:vectors] + out[vectors:]

    def split_tiles(c):
        tile_copies[c].wait()

        def step(i, carry):
            for j in range(2):
                t = c * chunk + 2 * i + j
                high, low = split(raw[t])
                halves[t, 0:tile, :] = high
                halves[t, tile : 2 * tile, :] = low
            return carry

        lax.fori_loop(0, chunk // 2, step, 0)

    def diagonal(source, target, target_base):
        def step(g, carry):
            for i in range(8):
                r = g * 8 + i
                target[target_base + r] = product(source[reach + r], r)
            return carry

        lax.fori_loop(0, row_tiles // 8, step, 0)

    def tables():
        for copy in int_copies:
            copy.wait()
        live = count_ref[0]
        base_col = position * row_tiles - reach
        base_row = position * row_tiles
        at = []
        for t in range(spare):
            index_ref[t] = jnp.clip(cols_ref[row_tiles + t] - base_col, 0, 2 * row_tiles - 1)
            row = jnp.where(row_tiles + t < live, rows_ref[row_tiles + t] - base_row, -1)
            link = jnp.int32(0)
            for s in range(t):
                link = jnp.where(at[s] == row, s + 1, link)
            before_ref[t] = link
            at.append(row)
        for r in range(row_tiles):
            link = jnp.int32(0)
            for s in range(spare):
                link = jnp.where(at[s] == r, s + 1, link)
            last_ref[r] = link

    def scattered(padded, target, target_base):
        for t in range(spare):
            out = product(padded[index_ref[t]], row_tiles + t)
            seg[t + 1] = out + seg[before_ref[t]]
        for r in range(row_tiles):
            target[target_base + r] = target[target_base + r] + seg[last_ref[r]]

    def parts(buffer, start):
        pieces = [split(buffer[start + t]) for t in range(row_tiles)]
        return [jnp.concatenate([piece[half] for piece in pieces], axis=1) for half in range(2)]

    def inner(left, right):
        lhs = jnp.concatenate([v[0] for v in left] + [v[1] for v in left], axis=0)
        rhs = jnp.concatenate([v[0] for v in right] + [v[1] for v in right], axis=0)
        out = lax.dot_general(lhs, rhs, NT_DIMS, preferred_element_type=F32)
        count = len(left) * vectors
        return out[:count] + out[count:]

    edge_lane = iota((EDGE, 128), 1)

    def pack(values, lanes):
        rows = values.shape[0]
        padded = jnp.concatenate([values, jnp.zeros((rows, 128 - 2 * lanes), F32)], axis=1)
        pieces = []
        for k in range(rows // EDGE):
            piece = padded[k * EDGE : (k + 1) * EDGE]
            first = piece if k == 0 else pltpu.roll(piece, k * lanes, 1)
            second = pltpu.roll(piece, (k * lanes - lanes) % 128, 1)
            here_lane = (edge_lane >= k * lanes) & (edge_lane < (k + 1) * lanes)
            pieces.append(jnp.where(here_lane, first + second, 0.0))
        return tree_sum(pieces)

    def unpack(values, rows, lanes):
        pieces = [
            values if k == 0 else pltpu.roll(values, 128 - k * lanes, 1) for k in range(rows // EDGE)
        ]
        return jnp.concatenate(pieces, axis=0)

    def exchange(which, values):
        mine[which] = values
        each_peer(
            lambda device: pltpu.make_async_remote_copy(
                src_ref=mine.at[which],
                dst_ref=every.at[which, position],
                send_sem=all_send.at[which],
                recv_sem=all_recv.at[which],
                device_id=device,
                device_id_type=MESH,
            ).start()
        )
        every[which, position] = values

    others = pl.ds(0, total - 1)

    def all_wait(which, sem):
        pltpu.make_async_copy(
            every.at[which, others], every.at[which, others], sem.at[which]
        ).wait()

    def collect(which):
        all_wait(which, all_recv)
        if total <= 32:
            return tree_sum([every[which, k] for k in range(total)])
        return lax.fori_loop(
            1, total, lambda k, out: out + every[which, k], every[which, 0]
        )

    tables()
    seg[0] = jnp.zeros((vectors, tile), F32)
    for c in range(chunks):
        split_tiles(c)
        if c == row_tiles // chunk - 1:
            diagonal(xh, yh, reach)
    diagonal(ph, q_buf, 0)
    x_parts, p_parts = parts(xh, reach), parts(ph, reach)
    exchange(0, pack(inner((x_parts, p_parts), (x_parts, p_parts)), 2 * vectors))

    halo_arrived(x_halo)
    scattered(xh, yh, reach)
    halo_start(y_halo)
    y_parts = parts(yh, reach)
    basis = (x_parts, y_parts, p_parts)
    exchange(1, pack(inner(basis, (y_parts,)), vectors))

    halo_arrived(p_halo)
    scattered(ph, q_buf, 0)
    exchange(2, pack(inner(basis, (parts(q_buf, 0),)), vectors))
    diagonal(yh, z_buf, 0)
    halo_arrived(y_halo)
    scattered(yh, z_buf, 0)
    exchange(3, pack(inner(basis, (parts(z_buf, 0),)), vectors))

    scale = 1.0 / vertex_total
    locked = locked_ref[0]
    by_xp = unpack(collect(0), 2 * vectors, 2 * vectors)
    by_y = unpack(collect(1), width, vectors)
    lane_w = iota((vectors, 128), 1)
    line_w = iota((vectors, 128), 0)
    middle_w = (lane_w >= vectors) & (lane_w < 2 * vectors)
    shifted_y = pltpu.roll(by_y, vectors, 1)
    shifted_xp = pltpu.roll(by_xp, vectors, 1)
    on_first = lane_w == line_w
    on_second = lane_w == line_w + vectors
    free_down = iota((vectors, 1), 0) >= locked
    free_along = (iota((1, 128), 1) >= vectors + locked) & (iota((1, 128), 1) < 2 * vectors)

    def diagonal_of(mask, values, axis):
        return jnp.sum(jnp.where(mask, values, 0.0), axis=axis, keepdims=True)

    def ratio(mask, over, under, axis):
        return (diagonal_of(mask, over, axis) + 1e-06) / (diagonal_of(mask, under, axis) + 1e-06)

    down = jnp.where(free_down, ratio(on_first, by_y[:vectors], by_xp[:vectors], 1), 0.0)
    along = jnp.where(
        free_along, ratio(on_second, shifted_y[:vectors], shifted_xp[:vectors], 0), 0.0
    )

    lane = iota((width, 128), 1)
    line = iota((width, 128), 0)
    is_first = lane < vectors
    is_second = (lane >= vectors) & (lane < 2 * vectors)
    is_third = (lane >= 2 * vectors) & (lane < width)
    square = jnp.concatenate(
        [jnp.where(lane < vectors, by_y, 0.0), jnp.zeros((128 - width, 128), F32)], axis=0
    )
    y_rows = jnp.transpose(square)[:vectors]
    zero_w = jnp.zeros((vectors, 128), F32)
    over_x = jnp.concatenate([by_xp[:vectors], y_rows, by_xp[vectors:]], axis=0)
    over_x_next = jnp.concatenate(
        [shifted_xp[:vectors], pltpu.roll(y_rows, vectors, 1), shifted_xp[vectors:]], axis=0
    )
    over_p = jnp.concatenate([shifted_xp[:vectors], y_rows, shifted_xp[vectors:]], axis=0)
    gate = jnp.where(free_along, 1.0, 0.0)

    def residual_rows(values):
        first, second, third = [values[i * vectors : (i + 1) * vectors] for i in range(3)]
        return jnp.concatenate(
            [first, jnp.where(free_down, down * first - second, 0.0), third], axis=0
        )

    def three(first, second, third):
        return jnp.where(
            is_first, first, jnp.where(is_second, second, jnp.where(is_third, third, 0.0))
        )

    gram = residual_rows(
        three(over_x, over_x_next * along - shifted_y * gate, over_p)
    )
    gram = gram * scale

    rest = gram[vectors : 2 * vectors]
    frozen = on_second & (line_w < locked)
    small = jnp.where(middle_w, rest + jnp.where(frozen, 1.0, 0.0), 0.0)
    small = small + jnp.where(lane_w == line_w + 2 * vectors, 1.0, 0.0)
    padded = (line == lane) & (line >= vectors) & (line < vectors + locked)
    big = gram + jnp.where(padded | (lane == line + width), 1.0, 0.0)

    step = 4
    small_rows = []
    for k in range(0, vectors, step):
        small, done = panel(small, k, vectors, step)
        small_rows += done
    inverse_w = jnp.concatenate(small_rows, axis=0)[:, 2 * vectors : 3 * vectors]

    def outputs():
        high, low = split(inverse_w)
        lhs = jnp.concatenate(
            [jnp.concatenate([high, high], axis=1), jnp.concatenate([low, low], axis=1)], axis=0
        )

        def turn(values):
            rhs = jnp.concatenate(split(values), axis=0)
            out = jnp.dot(lhs, rhs, preferred_element_type=F32)
            return out[:vectors] + out[vectors:]

        for t in range(row_tiles):
            lanes = slice(t * tile, (t + 1) * tile)
            image = yh[reach + t]
            residual = jnp.where(free_down, down * xh[reach + t] - image, 0.0)
            carried = jnp.where(free_down, down * image - z_buf[t], 0.0)
            w_ref[:, lanes] = turn(residual)
            aw_ref[:, lanes] = turn(residual - carried)

    for k in range(0, width, step):
        if k == 2 * vectors:
            outputs()
        big, done = panel(big, k, 0, step)
        for i in range(step):
            upper[k + i : k + i + 1, :] = done[i]
    inverse = upper[:, width : 2 * width]

    by_q = unpack(collect(2), width, vectors)
    early = residual_rows(three(by_y, shifted_y * along, pltpu.roll(by_q, 2 * vectors, 1)))
    by_z = unpack(collect(3), width, vectors)
    late = residual_rows(jnp.where(is_second, pltpu.roll(by_z, vectors, 1) * gate, 0.0))
    image = (gram - scale * (early - late))[:, :width]
    half = jnp.dot(inverse, image, precision=HIGHEST, preferred_element_type=F32)
    first = lax.dot_general(half, inverse, NT_DIMS, precision=HIGHEST, preferred_element_type=F32)
    second = lax.dot_general(inverse, half, NT_DIMS, precision=HIGHEST, preferred_element_type=F32)
    ritz_ref[...] = 0.5 * (first + second)

    halo_sent(x_halo)
    halo_sent(p_halo)
    halo_sent(y_halo)
    for which in range(4):
        all_wait(which, all_send)


def store_kernel(w_ref, aw_ref, ritz_ref, w_hbm, aw_hbm, ritz_hbm, sem):
    copies = [
        pltpu.make_async_copy(source, target, sem.at[i])
        for i, (source, target) in enumerate(
            ((w_ref, w_hbm), (aw_ref, aw_hbm), (ritz_ref, ritz_hbm))
        )
    ]
    for copy in copies:
        copy.start()
    for copy in copies:
        copy.wait()


def body(sizes, current_block, previous_block, adjacency_tiles, tile_rows, tile_cols, tile_count, locked):
    vectors, here = current_block.shape
    slots, tile, _ = adjacency_tiles.shape
    row_tiles = here // tile
    row_count, col_count, sub_count = sizes
    total = row_count * col_count * sub_count
    width = 3 * vectors
    spare = slots - row_tiles
    vmem = pl.BlockSpec(memory_space=pltpu.VMEM)
    anywhere = pl.BlockSpec(memory_space=pl.ANY)
    dma = pltpu.SemaphoreType.DMA
    grid = (2 * row_tiles, vectors, tile)
    own = (row_tiles, vectors, tile)
    shapes = (
        jax.ShapeDtypeStruct((vectors, here), F32),
        jax.ShapeDtypeStruct((vectors, here), F32),
        jax.ShapeDtypeStruct((width, width), F32),
    )
    results = pl.pallas_call(
        functools.partial(iterate_kernel, sizes, here * total),
        out_shape=shapes,
        in_specs=[anywhere] * 7,
        out_specs=(vmem, vmem, vmem),
        scratch_shapes=[
            pltpu.SMEM((slots,), jnp.int32),
            pltpu.SMEM((slots,), jnp.int32),
            pltpu.SMEM((1,), jnp.int32),
            pltpu.SMEM((1,), jnp.int32),
            pltpu.SMEM((spare,), jnp.int32),
            pltpu.SMEM((spare,), jnp.int32),
            pltpu.SMEM((row_tiles,), jnp.int32),
            pltpu.VMEM((slots, tile, tile), F32),
            pltpu.VMEM((slots, 2 * tile, tile), BF16),
            pltpu.VMEM(grid, F32),
            pltpu.VMEM(grid, F32),
            pltpu.VMEM(grid, F32),
            pltpu.VMEM(own, F32),
            pltpu.VMEM(own, F32),
            pltpu.VMEM((spare + 1, vectors, tile), F32),
            pltpu.VMEM((4, EDGE, 128), F32),
            pltpu.VMEM((4, total, EDGE, 128), F32),
            pltpu.VMEM((width, 128), F32),
            dma((4,)),
            dma((2,)),
            dma((slots // row_tiles,)),
            dma((3, 2)),
            dma((3, 2)),
            dma((4,)),
            dma((4,)),
        ],
        compiler_params=pltpu.CompilerParams(
            collective_id=0, has_side_effects=True, vmem_limit_bytes=VMEM_ALL - VMEM_ROOM
        ),
        name="iterate",
    )(tile_cols, tile_rows, tile_count, locked, current_block, previous_block, adjacency_tiles)
    return pl.pallas_call(
        store_kernel,
        out_shape=shapes,
        in_specs=[vmem] * 3,
        out_specs=(anywhere,) * 3,
        scratch_shapes=[dma((3,))],
        compiler_params=pltpu.CompilerParams(vmem_limit_bytes=VMEM_ALL - VMEM_ROOM),
        name="store",
    )(*results)


def solution(mesh):
    split_all = ("graphs", "rows", "cols", "sub")
    sizes = tuple(mesh.shape[name] for name in ("rows", "cols", "sub"))
    in_specs = (
        P(None, split_all),
        P(None, split_all),
        P(split_all, None, None),
        P(split_all),
        P(split_all),
        P(split_all),
        P("graphs"),
    )
    out_specs = (P(None, split_all), P(None, split_all), P("graphs", None))
    return jax.shard_map(
        functools.partial(body, sizes), mesh=mesh, in_specs=in_specs, out_specs=out_specs, check_vma=False
    )
```

time: 30.2 us -> 23.2 us (0.77)
  Pallas kernels: 28 us -> 19.8 us
  local copies, waits for them, and re-layouts: 0 us -> 1.3 us
    pallas_call x2, Pallas kernels: 28 us -> 19.8 us  [the longest x1 19.1 us: body(): pl.pallas_call(functools.partial(iterate_kernel, sizes, here * total), ou...]
    unnamed x0 -> x4, local copies, waits for them, and re-layouts: none -> 1.3 us
where the time goes in v1:
time: 23.2 us; the launch traced here: 23 us
  Pallas kernels  19.8 us (85%)
  between operations  1.94 us (8%)
  local copies, waits for them, and re-layouts  1.3 us (6%)
    pallas_call x1, Pallas kernels, body(): pl.pallas_call(functools.partial(iterate_kernel, sizes, here * total), ou...  19.1 us
    unnamed x4, local copies, waits for them, and re-layouts  1.3 us
    pallas_call x1, Pallas kernels, body(): pl.pallas_call(store_kernel, out_shape=shapes, in_specs=[vmem] * 3, out_s...  0.73 us

profile of v1, /device:TPU:0, one launch (start us, length us, event | category | flops | bytes accessed | tf_op | source)
XLA Modules:
  0.0 23.0 jit_solution(2164833728637132245)
XLA Ops:
  1.9 0.0 copy-start
  1.9 0.6 %copy-done = s32[48]{0:T(128)S(1)} copy-done((s32[48]{0:T(128)S(1)}, s32[48]{0:T(128)}, u32[]{:S(2)}) %copy-start) | copy-done | bytes 216
  2.6 0.0 copy-start.1
  2.6 0.7 %copy-done.1 = s32[48]{0:T(128)S(1)} copy-done((s32[48]{0:T(128)S(1)}, s32[48]{0:T(128)}, u32[]{:S(2)}) %copy-start.1) | copy-done | bytes 216
  3.2 19.1 %iterate.1 = (f32[16,2048]{1,0:T(8,128)S(1)}, f32[16,2048]{1,0:T(8,128)S(1)}, f32[48,48]{1,0:T(8,128)S(1)}) custom-call(s32[48]{0:T(128)S(1)} %copy-done, s32[48]{0:T(128)S(1)} %copy-done.1, s32[1]{0:T(128)S(6)} %copy.10.count_in, s32[1]{0:T(128)S(6)} %copy.11.locked_in, f32[16,2048]{1,0:T(8,128)} %x_hbm.1, f32[16,2048]{1,0:T(8,128)} %p_hbm.1, ...), custom_call_target="tpu_custom_call" | custom-call | tf_op jit(solution)/shard_map/iterate/pallas_call | solution.py:495
  22.3 0.7 %store.1 = (f32[16,2048]{1,0:T(8,128)}, f32[16,2048]{1,0:T(8,128)}, f32[48,48]{1,0:T(8,128)}) custom-call(f32[16,2048]{1,0:T(8,128)S(1)} %get-tuple-element.6.w_ref, f32[16,2048]{1,0:T(8,128)S(1)} %get-tuple-element.7.aw_ref, f32[48,48]{1,0:T(8,128)S(1)} %get-tuple-element.8.ritz_ref), custom_call_target="tpu_custom_call" | custom-call | tf_op jit(solution)/shard_map/store/pallas_call | solution.py:532
Async XLA Ops:
  1.9 0.7 %copy-start = (s32[48]{0:T(128)S(1)}, s32[48]{0:T(128)}, u32[]{:S(2)}) copy-start(s32[48]{0:T(128)} %cols_in.1) | copy-start | bytes 580
  2.6 0.7 %copy-start.1 = (s32[48]{0:T(128)S(1)}, s32[48]{0:T(128)}, u32[]{:S(2)}) copy-start(s32[48]{0:T(128)} %rows_in.1) | copy-start | bytes 580

commit v2 on v1

--- a/solution.py
+++ b/solution.py
@@ -59,11 +59,12 @@
 
 def iterate_kernel(
     sizes, vertex_total,
-    cols_in, rows_in, count_in, locked_in, x_hbm, p_hbm, tiles_hbm,
+    ints_hbm, x_hbm, p_hbm, tiles_hbm,
     w_ref, aw_ref, ritz_ref,
-    cols_ref, rows_ref, count_ref, locked_ref, index_ref, before_ref, last_ref,
-    raw, halves, xh, ph, yh, q_buf, z_buf, seg, mine, every, upper,
-    int_sem, block_sem, tile_sem, halo_send, halo_recv, all_send, all_recv,
+    ints_ref, index_ref, before_ref, last_ref,
+    raw, halves, xh, ph, yh, q_buf, z_buf, seg, near_ref, far_ref, every, upper,
+    int_sem, block_sem, tile_sem, halo_send, halo_recv, near_send, near_recv, far_send, far_recv,
+    all_send, all_recv,
 ):
     row_count, col_count, sub_count = sizes
     near_count = col_count * sub_count
@@ -128,19 +129,8 @@
         pltpu.make_async_copy(target.at[own], target.at[own], sem).wait()
 
     block_start(x_hbm, xh, block_sem.at[0])
-    int_copies = [
-        pltpu.make_async_copy(source, target, int_sem.at[i])
-        for i, (source, target) in enumerate(
-            (
-                (cols_in, cols_ref),
-                (rows_in, rows_ref),
-                (count_in, count_ref),
-                (locked_in, locked_ref),
-            )
-        )
-    ]
-    for copy in int_copies:
-        copy.start()
+    int_copy = pltpu.make_async_copy(ints_hbm, ints_ref, int_sem.at[0])
+    int_copy.start()
     tile_copies = []
     for c in range(chunks):
         part = pl.ds(c * chunk, chunk)
@@ -199,8 +189,6 @@
     block_wait(xh, block_sem.at[0])
     pl.semaphore_wait(barrier, total - 1)
     halo_start(x_halo)
-    block_wait(ph, block_sem.at[1])
-    halo_start(p_halo)
 
     def product(block, slot):
         high, low = split(block)
@@ -233,15 +221,14 @@
         lax.fori_loop(0, row_tiles // 8, step, 0)
 
     def tables():
-        for copy in int_copies:
-            copy.wait()
-        live = count_ref[0]
+        int_copy.wait()
+        live = ints_ref[2 * slots]
         base_col = position * row_tiles - reach
         base_row = position * row_tiles
         at = []
         for t in range(spare):
-            index_ref[t] = jnp.clip(cols_ref[row_tiles + t] - base_col, 0, 2 * row_tiles - 1)
-            row = jnp.where(row_tiles + t < live, rows_ref[row_tiles + t] - base_row, -1)
+            index_ref[t] = jnp.clip(ints_ref[row_tiles + t] - base_col, 0, 2 * row_tiles - 1)
+            row = jnp.where(row_tiles + t < live, ints_ref[slots + row_tiles + t] - base_row, -1)
             link = jnp.int32(0)
             for s in range(t):
                 link = jnp.where(at[s] == row, s + 1, link)
@@ -291,64 +278,98 @@
         ]
         return jnp.concatenate(pieces, axis=0)
 
-    def exchange(which, values):
-        mine[which] = values
-        each_peer(
-            lambda device: pltpu.make_async_remote_copy(
-                src_ref=mine.at[which],
-                dst_ref=every.at[which, position],
-                send_sem=all_send.at[which],
-                recv_sem=all_recv.at[which],
-                device_id=device,
-                device_id_type=MESH,
-            ).start()
-        )
-        every[which, position] = values
-
-    others = pl.ds(0, total - 1)
-
-    def all_wait(which, sem):
-        pltpu.make_async_copy(
-            every.at[which, others], every.at[which, others], sem.at[which]
-        ).wait()
-
-    def collect(which):
-        all_wait(which, all_recv)
+    def stage(buffer, which, height, count, at, device, send, recv):
+        def start(*values):
+            mine = buffer.at[which, at, pl.ds(0, height)]
+            for k, value in enumerate(values):
+                buffer[which, at, k * EDGE : (k + 1) * EDGE] = value
+            for k in range(1, count):
+                pltpu.make_async_remote_copy(
+                    src_ref=mine,
+                    dst_ref=mine,
+                    send_sem=send.at[which],
+                    recv_sem=recv.at[which],
+                    device_id=device(k),
+                    device_id_type=MESH,
+                ).start()
+
+        def wait(sem):
+            rest = buffer.at[which, pl.ds(0, count - 1), pl.ds(0, height)]
+            pltpu.make_async_copy(rest, rest, sem.at[which]).wait()
+
+        def collect():
+            wait(recv)
+            return tree_sum([buffer[which, k, 0:height] for k in range(count)])
+
+        return start, collect, lambda: wait(send)
+
+    def near_device(k):
+        return {"cols": cols_from[k // sub_count], "sub": subs_from[k % sub_count]}
+
+    def far_device(k):
+        return {"rows": rows_from[k]}
+
+    def any_device(k):
+        return far_device(k // near_count) | near_device(k % near_count)
+
+    near_at = col_at * sub_count + sub_at
+
+    def near_stage(which):
+        return stage(near_ref, which, EDGE, near_count, near_at, near_device, near_send, near_recv)
+
+    def far_stage(which):
+        return stage(far_ref, which, EDGE, row_count, row_at, far_device, far_send, far_recv)
+
+    def all_stage(which):
         if total <= 32:
-            return tree_sum([every[which, k] for k in range(total)])
-        return lax.fori_loop(
-            1, total, lambda k, out: out + every[which, k], every[which, 0]
-        )
+            return stage(every, which, EDGE, total, position, any_device, all_send, all_recv)
+        first, second = near_stage(which + 1), far_stage(which + 1)
+
+        def start(values):
+            first[0](values)
+            second[0](first[1]())
+
+        def sent():
+            first[2]()
+            second[2]()
+
+        return start, second[1], sent
+
+    near_x, far_x = near_stage(0), far_stage(0)
+    all_y, all_q, all_z = all_stage(0), all_stage(1), all_stage(2)
 
     tables()
+    block_wait(ph, block_sem.at[1])
     seg[0] = jnp.zeros((vectors, tile), F32)
     for c in range(chunks):
         split_tiles(c)
         if c == row_tiles // chunk - 1:
             diagonal(xh, yh, reach)
+    halo_start(p_halo)
     diagonal(ph, q_buf, 0)
     x_parts, p_parts = parts(xh, reach), parts(ph, reach)
-    exchange(0, pack(inner((x_parts, p_parts), (x_parts, p_parts)), 2 * vectors))
+    near_x[0](pack(inner((x_parts, p_parts), (x_parts, p_parts)), 2 * vectors))
 
     halo_arrived(x_halo)
     scattered(xh, yh, reach)
     halo_start(y_halo)
     y_parts = parts(yh, reach)
     basis = (x_parts, y_parts, p_parts)
-    exchange(1, pack(inner(basis, (y_parts,)), vectors))
-
+    all_y[0](pack(inner(basis, (y_parts,)), vectors))
+
+    far_x[0](near_x[1]())
     halo_arrived(p_halo)
     scattered(ph, q_buf, 0)
-    exchange(2, pack(inner(basis, (parts(q_buf, 0),)), vectors))
+    all_q[0](pack(inner(basis, (parts(q_buf, 0),)), vectors))
     diagonal(yh, z_buf, 0)
     halo_arrived(y_halo)
     scattered(yh, z_buf, 0)
-    exchange(3, pack(inner(basis, (parts(z_buf, 0),)), vectors))
+    all_z[0](pack(inner(basis, (parts(z_buf, 0),)), vectors))
 
     scale = 1.0 / vertex_total
-    locked = locked_ref[0]
-    by_xp = unpack(collect(0), 2 * vectors, 2 * vectors)
-    by_y = unpack(collect(1), width, vectors)
+    locked = ints_ref[2 * slots + 1]
+    by_xp = unpack(far_x[1](), 2 * vectors, 2 * vectors)
+    by_y = unpack(all_y[1](), width, vectors)
     lane_w = iota((vectors, 128), 1)
     line_w = iota((vectors, 128), 0)
     middle_w = (lane_w >= vectors) & (lane_w < 2 * vectors)
@@ -444,9 +465,9 @@
             upper[k + i : k + i + 1, :] = done[i]
     inverse = upper[:, width : 2 * width]
 
-    by_q = unpack(collect(2), width, vectors)
+    by_q = unpack(all_q[1](), width, vectors)
     early = residual_rows(three(by_y, shifted_y * along, pltpu.roll(by_q, 2 * vectors, 1)))
-    by_z = unpack(collect(3), width, vectors)
+    by_z = unpack(all_z[1](), width, vectors)
     late = residual_rows(jnp.where(is_second, pltpu.roll(by_z, vectors, 1) * gate, 0.0))
     image = (gram - scale * (early - late))[:, :width]
     half = jnp.dot(inverse, image, precision=HIGHEST, preferred_element_type=F32)
@@ -457,8 +478,8 @@
     halo_sent(x_halo)
     halo_sent(p_halo)
     halo_sent(y_halo)
-    for which in range(4):
-        all_wait(which, all_send)
+    for done in (near_x, far_x, all_y, all_q, all_z):
+        done[2]()
 
 
 def store_kernel(w_ref, aw_ref, ritz_ref, w_hbm, aw_hbm, ritz_hbm, sem):
@@ -479,7 +500,8 @@
     slots, tile, _ = adjacency_tiles.shape
     row_tiles = here // tile
     row_count, col_count, sub_count = sizes
-    total = row_count * col_count * sub_count
+    near_count = col_count * sub_count
+    total = row_count * near_count
     width = 3 * vectors
     spare = slots - row_tiles
     vmem = pl.BlockSpec(memory_space=pltpu.VMEM)
@@ -492,16 +514,17 @@
         jax.ShapeDtypeStruct((vectors, here), F32),
         jax.ShapeDtypeStruct((width, width), F32),
     )
+    used = 2 * slots + 2
+    ints = jnp.concatenate(
+        [tile_cols, tile_rows, tile_count, locked, jnp.zeros((-used % 128,), jnp.int32)]
+    )
     results = pl.pallas_call(
         functools.partial(iterate_kernel, sizes, here * total),
         out_shape=shapes,
-        in_specs=[anywhere] * 7,
+        in_specs=[anywhere] * 4,
         out_specs=(vmem, vmem, vmem),
         scratch_shapes=[
-            pltpu.SMEM((slots,), jnp.int32),
-            pltpu.SMEM((slots,), jnp.int32),
-            pltpu.SMEM((1,), jnp.int32),
-            pltpu.SMEM((1,), jnp.int32),
+            pltpu.SMEM(ints.shape, jnp.int32),
             pltpu.SMEM((spare,), jnp.int32),
             pltpu.SMEM((spare,), jnp.int32),
             pltpu.SMEM((row_tiles,), jnp.int32),
@@ -513,22 +536,27 @@
             pltpu.VMEM(own, F32),
             pltpu.VMEM(own, F32),
             pltpu.VMEM((spare + 1, vectors, tile), F32),
-            pltpu.VMEM((4, EDGE, 128), F32),
-            pltpu.VMEM((4, total, EDGE, 128), F32),
+            pltpu.VMEM((4, near_count, EDGE, 128), F32),
+            pltpu.VMEM((4, row_count, EDGE, 128), F32),
+            pltpu.VMEM((3, total, EDGE, 128), F32),
             pltpu.VMEM((width, 128), F32),
-            dma((4,)),
+            dma((1,)),
             dma((2,)),
             dma((slots // row_tiles,)),
             dma((3, 2)),
             dma((3, 2)),
             dma((4,)),
             dma((4,)),
+            dma((4,)),
+            dma((4,)),
+            dma((3,)),
+            dma((3,)),
         ],
         compiler_params=pltpu.CompilerParams(
             collective_id=0, has_side_effects=True, vmem_limit_bytes=VMEM_ALL - VMEM_ROOM
         ),
         name="iterate",
-    )(tile_cols, tile_rows, tile_count, locked, current_block, previous_block, adjacency_tiles)
+    )(ints, current_block, previous_block, adjacency_tiles)
     return pl.pallas_call(
         store_kernel,
         out_shape=shapes,

time: 23.2 us -> 21.5 us (0.927)
  Pallas kernels: 19.8 us -> 18.6 us
  local copies, waits for them, and re-layouts: 1.3 us -> 0.75 us
    unnamed x4 -> x0, local copies, waits for them, and re-layouts: 1.3 us -> none
    pallas_call x1, Pallas kernels: 19.1 us -> 17.9 us  [body(): pl.pallas_call(functools.partial(iterate_kernel, sizes, here * total), ou...]
    concatenate x0 -> x1, local copies, waits for them, and re-layouts: none -> 0.75 us  [body(): jnp.concatenate([tile_cols, tile_rows, tile_count, locked, jnp.zeros((-us...]
where the time goes in v2:
time: 21.5 us; the launch traced here: 21.3 us
  Pallas kernels  18.6 us (87%)
  between operations  1.94 us (9%)
  local copies, waits for them, and re-layouts  0.75 us (3%)
    pallas_call x1, Pallas kernels, body(): pl.pallas_call(functools.partial(iterate_kernel, sizes, here * total), ou...  17.9 us
    concatenate x1, local copies, waits for them, and re-layouts, body(): jnp.concatenate([tile_cols, tile_rows, tile_count, locked, jnp.zeros((-us...  0.75 us
    pallas_call x1, Pallas kernels, body(): pl.pallas_call(store_kernel, out_shape=shapes, in_specs=[vmem] * 3, out_s...  0.73 us

profile of v2, /device:TPU:0, one launch (start us, length us, event | category | flops | bytes accessed | tf_op | source)
XLA Modules:
  0.0 21.3 jit_solution(9645236637054566818)
XLA Ops:
  1.9 0.8 %concatenate.3.ints_hbm = s32[128]{0:T(128)S(1)} concatenate(s32[48]{0:T(128)} %param.11, s32[48]{0:T(128)} %param.10, s32[1]{0:T(128)S(6)} %copy.10, s32[1]{0:T(128)S(6)} %copy.11, s32[30]{0:T(128)S(1)} %broadcast.3), dimensions={0} | concatenate | bytes 1024 | tf_op jit(solution)/shard_map/concatenate | solution.py:518
  2.7 17.9 %iterate.1 = (f32[16,2048]{1,0:T(8,128)S(1)}, f32[16,2048]{1,0:T(8,128)S(1)}, f32[48,48]{1,0:T(8,128)S(1)}) custom-call(s32[128]{0:T(128)S(1)} %concatenate.3.ints_hbm, f32[16,2048]{1,0:T(8,128)} %x_hbm.1, f32[16,2048]{1,0:T(8,128)} %p_hbm.1, f32[48,128,128]{2,1,0:T(8,128)} %tiles_hbm.1), custom_call_target="tpu_custom_call" | custom-call | tf_op jit(solution)/shard_map/iterate/pallas_call | solution.py:521
  20.6 0.7 %store.1 = (f32[16,2048]{1,0:T(8,128)}, f32[16,2048]{1,0:T(8,128)}, f32[48,48]{1,0:T(8,128)}) custom-call(f32[16,2048]{1,0:T(8,128)S(1)} %get-tuple-element.6.w_ref, f32[16,2048]{1,0:T(8,128)S(1)} %get-tuple-element.7.aw_ref, f32[48,48]{1,0:T(8,128)S(1)} %get-tuple-element.8.ritz_ref), custom_call_target="tpu_custom_call" | custom-call | tf_op jit(solution)/shard_map/store/pallas_call | solution.py:560
  (1 shorter events, 0.0 us)

commit v3 on v2

--- a/solution.py
+++ b/solution.py
@@ -64,7 +64,7 @@
     ints_ref, index_ref, before_ref, last_ref,
     raw, halves, xh, ph, yh, q_buf, z_buf, seg, near_ref, far_ref, every, upper,
     int_sem, block_sem, tile_sem, halo_send, halo_recv, near_send, near_recv, far_send, far_recv,
-    all_send, all_recv,
+    all_send, all_recv, relay,
 ):
     row_count, col_count, sub_count = sizes
     near_count = col_count * sub_count
@@ -94,28 +94,61 @@
     cols_from = [lax.rem(col_at + k, col_count) for k in range(col_count)]
     subs_from = [lax.rem(sub_at + k, sub_count) for k in range(sub_count)]
 
-    def each_peer(act):
-        if total <= 32:
-            for k in range(1, total):
-                act(
-                    {
-                        "rows": rows_from[k // near_count],
-                        "cols": cols_from[k % near_count // sub_count],
-                        "sub": subs_from[k % sub_count],
-                    }
-                )
-        else:
-
-            def step(k, carry):
-                act(place(lax.rem(position + k, total)))
-                return carry
-
-            lax.fori_loop(1, total, step, 0)
+    has_left = position > 0
+    has_right = position < total - 1
+    has_under = row_at > 0
+    has_over = row_at < row_count - 1
+    left_device = place(lax.max(position - 1, 0))
+    right_device = place(lax.min(position + 1, total - 1))
+    under_device = {"rows": lax.max(row_at - 1, 0)}
+    over_device = {"rows": lax.min(row_at + 1, row_count - 1)}
+    near_at = col_at * sub_count + sub_at
+    crosses_left = has_left & (near_at == 0)
+    crosses_right = has_right & (near_at == near_count - 1)
+
+    def near_device(k):
+        return {"cols": cols_from[k // sub_count], "sub": subs_from[k % sub_count]}
+
+    def far_device(k):
+        return {"rows": rows_from[k]}
+
+    def any_device(k):
+        return far_device(k // near_count) | near_device(k % near_count)
+
+    def signal(semaphore, device):
+        pl.semaphore_signal(semaphore, inc=1, device_id=device, device_id_type=MESH)
 
     barrier = pltpu.get_barrier_semaphore()
-    each_peer(
-        lambda device: pl.semaphore_signal(barrier, inc=1, device_id=device, device_id_type=MESH)
-    )
+    greeted = near_count - 1
+    for there, device in (
+        (crosses_left, left_device),
+        (crosses_right, right_device),
+        (has_under, under_device),
+        (has_over, over_device),
+    ):
+        pl.when(there)(functools.partial(signal, barrier, device))
+        greeted = greeted + jnp.where(there, 1, 0)
+    for k in range(1, near_count):
+        signal(barrier, near_device(k))
+
+    def tell():
+        pl.when(has_under)(functools.partial(signal, relay.at[1], under_device))
+        pl.when(has_over)(functools.partial(signal, relay.at[0], over_device))
+
+    def hear():
+        pl.when(has_under)(lambda: pl.semaphore_wait(relay.at[0], 1))
+        pl.when(has_over)(lambda: pl.semaphore_wait(relay.at[1], 1))
+
+    def hear_rest():
+        hear()
+
+        def step(k, carry):
+            tell()
+            hear()
+            return carry
+
+        if row_count > 4:
+            lax.fori_loop(0, row_count - 4, step, 0)
 
     own = pl.ds(reach, row_tiles)
 
@@ -139,11 +172,6 @@
     block_start(p_hbm, ph, block_sem.at[1])
     for copy in tile_copies[1:]:
         copy.start()
-
-    has_left = position > 0
-    has_right = position < total - 1
-    left_device = place(lax.max(position - 1, 0))
-    right_device = place(lax.min(position + 1, total - 1))
 
     def halo_copies(buffer, which):
         left = pltpu.make_async_remote_copy(
@@ -187,8 +215,9 @@
     y_halo = halo_copies(yh, 2)
 
     block_wait(xh, block_sem.at[0])
-    pl.semaphore_wait(barrier, total - 1)
+    pl.semaphore_wait(barrier, greeted)
     halo_start(x_halo)
+    tell()
 
     def product(block, slot):
         high, low = split(block)
@@ -303,17 +332,6 @@
 
         return start, collect, lambda: wait(send)
 
-    def near_device(k):
-        return {"cols": cols_from[k // sub_count], "sub": subs_from[k % sub_count]}
-
-    def far_device(k):
-        return {"rows": rows_from[k]}
-
-    def any_device(k):
-        return far_device(k // near_count) | near_device(k % near_count)
-
-    near_at = col_at * sub_count + sub_at
-
     def near_stage(which):
         return stage(near_ref, which, EDGE, near_count, near_at, near_device, near_send, near_recv)
 
@@ -339,17 +357,22 @@
     all_y, all_q, all_z = all_stage(0), all_stage(1), all_stage(2)
 
     tables()
+    hear()
+    tell()
     block_wait(ph, block_sem.at[1])
     seg[0] = jnp.zeros((vectors, tile), F32)
     for c in range(chunks):
         split_tiles(c)
         if c == row_tiles // chunk - 1:
             diagonal(xh, yh, reach)
+    hear()
+    tell()
     halo_start(p_halo)
     diagonal(ph, q_buf, 0)
     x_parts, p_parts = parts(xh, reach), parts(ph, reach)
     near_x[0](pack(inner((x_parts, p_parts), (x_parts, p_parts)), 2 * vectors))
 
+    hear_rest()
     halo_arrived(x_halo)
     scattered(xh, yh, reach)
     halo_start(y_halo)
@@ -551,6 +574,7 @@
             dma((4,)),
             dma((3,)),
             dma((3,)),
+            pltpu.SemaphoreType.REGULAR((2,)),
         ],
         compiler_params=pltpu.CompilerParams(
             collective_id=0, has_side_effects=True, vmem_limit_bytes=VMEM_ALL - VMEM_ROOM

time: 21.5 us -> 21.3 us (level)
  no operation moved by 1% of the time
where the time goes in v3:
time: 21.3 us; the launch traced here: 21.2 us
  Pallas kernels  18.5 us (87%)
  between operations  1.94 us (9%)
  local copies, waits for them, and re-layouts  0.75 us (4%)
    pallas_call x1, Pallas kernels, body(): pl.pallas_call(functools.partial(iterate_kernel, sizes, here * total), ou...  17.8 us
    concatenate x1, local copies, waits for them, and re-layouts, body(): jnp.concatenate([tile_cols, tile_rows, tile_count, locked, jnp.zeros((-us...  0.75 us
    pallas_call x1, Pallas kernels, body(): pl.pallas_call(store_kernel, out_shape=shapes, in_specs=[vmem] * 3, out_s...  0.73 us

profile of v3, /device:TPU:0, one launch (start us, length us, event | category | flops | bytes accessed | tf_op | source)
XLA Modules:
  0.0 21.2 jit_solution(12691767239862422961)
XLA Ops:
  1.9 0.8 %concatenate.3.ints_hbm = s32[128]{0:T(128)S(1)} concatenate(s32[48]{0:T(128)} %param.11, s32[48]{0:T(128)} %param.10, s32[1]{0:T(128)S(6)} %copy.10, s32[1]{0:T(128)S(6)} %copy.11, s32[30]{0:T(128)S(1)} %broadcast.3), dimensions={0} | concatenate | bytes 1024 | tf_op jit(solution)/shard_map/concatenate | solution.py:541
  2.7 17.8 %iterate.1 = (f32[16,2048]{1,0:T(8,128)S(1)}, f32[16,2048]{1,0:T(8,128)S(1)}, f32[48,48]{1,0:T(8,128)S(1)}) custom-call(s32[128]{0:T(128)S(1)} %concatenate.3.ints_hbm, f32[16,2048]{1,0:T(8,128)} %x_hbm.1, f32[16,2048]{1,0:T(8,128)} %p_hbm.1, f32[48,128,128]{2,1,0:T(8,128)} %tiles_hbm.1), custom_call_target="tpu_custom_call" | custom-call | tf_op jit(solution)/shard_map/iterate/pallas_call | solution.py:544
  20.4 0.7 %store.1 = (f32[16,2048]{1,0:T(8,128)}, f32[16,2048]{1,0:T(8,128)}, f32[48,48]{1,0:T(8,128)}) custom-call(f32[16,2048]{1,0:T(8,128)S(1)} %get-tuple-element.6.w_ref, f32[16,2048]{1,0:T(8,128)S(1)} %get-tuple-element.7.aw_ref, f32[48,48]{1,0:T(8,128)S(1)} %get-tuple-element.8.ritz_ref), custom_call_target="tpu_custom_call" | custom-call | tf_op jit(solution)/shard_map/store/pallas_call | solution.py:584
  (1 shorter events, 0.0 us)

commit v4 on v3

--- a/solution.py
+++ b/solution.py
@@ -113,7 +113,13 @@
         return {"rows": rows_from[k]}
 
     def any_device(k):
-        return far_device(k // near_count) | near_device(k % near_count)
+        turn = (k - 1) // near_count
+        if turn == row_count - 1:
+            return near_device(k - turn * near_count)
+        up = turn + jnp.where(turn >= row_at, 1, 0)
+        down = row_count - 1 - turn
+        down = down - jnp.where(down <= row_at, 1, 0)
+        return {"rows": jnp.where(2 * row_at >= row_count, up, down)} | near_device((k - 1) % near_count)
 
     def signal(semaphore, device):
         pl.semaphore_signal(semaphore, inc=1, device_id=device, device_id_type=MESH)
@@ -283,9 +289,13 @@
     def inner(left, right):
         lhs = jnp.concatenate([v[0] for v in left] + [v[1] for v in left], axis=0)
         rhs = jnp.concatenate([v[0] for v in right] + [v[1] for v in right], axis=0)
-        out = lax.dot_general(lhs, rhs, NT_DIMS, preferred_element_type=F32)
+        half = here // 2
+        out = [
+            lax.dot_general(lhs[:, part], rhs[:, part], NT_DIMS, preferred_element_type=F32)
+            for part in (slice(0, half), slice(half, here))
+        ]
         count = len(left) * vectors
-        return out[:count] + out[count:]
+        return (out[0][:count] + out[1][:count]) + (out[0][count:] + out[1][count:])
 
     edge_lane = iota((EDGE, 128), 1)
 
@@ -301,9 +311,10 @@
             pieces.append(jnp.where(here_lane, first + second, 0.0))
         return tree_sum(pieces)
 
-    def unpack(values, rows, lanes):
+    def unpack(values, rows, lanes, at=0):
         pieces = [
-            values if k == 0 else pltpu.roll(values, 128 - k * lanes, 1) for k in range(rows // EDGE)
+            values if k * lanes == at else pltpu.roll(values, (at - k * lanes) % 128, 1)
+            for k in range(rows // EDGE)
         ]
         return jnp.concatenate(pieces, axis=0)
 
@@ -488,15 +499,31 @@
             upper[k + i : k + i + 1, :] = done[i]
     inverse = upper[:, width : 2 * width]
 
-    by_q = unpack(all_q[1](), width, vectors)
-    early = residual_rows(three(by_y, shifted_y * along, pltpu.roll(by_q, 2 * vectors, 1)))
-    by_z = unpack(all_z[1](), width, vectors)
-    late = residual_rows(jnp.where(is_second, pltpu.roll(by_z, vectors, 1) * gate, 0.0))
-    image = (gram - scale * (early - late))[:, :width]
+    by_q = unpack(all_q[1](), width, vectors, 2 * vectors)
+    early = residual_rows(three(by_y, shifted_y * along, by_q))
+    image = (gram - scale * early)[:, :width]
     half = jnp.dot(inverse, image, precision=HIGHEST, preferred_element_type=F32)
     first = lax.dot_general(half, inverse, NT_DIMS, precision=HIGHEST, preferred_element_type=F32)
     second = lax.dot_general(inverse, half, NT_DIMS, precision=HIGHEST, preferred_element_type=F32)
-    ritz_ref[...] = 0.5 * (first + second)
+    base = first + second
+    inverse_high, inverse_low = split(inverse)
+    left = jnp.concatenate([inverse_high, inverse_low, inverse_high], axis=1)
+    right = jnp.concatenate([inverse_high, inverse_high, inverse_low], axis=1)
+
+    by_z = unpack(all_z[1](), width, vectors, vectors)
+    late = residual_rows(by_z)[:, :width]
+    late = jnp.where(is_second[:, :width], late, 0.0) * gate[:, :width]
+    late_high, late_low = split(late * scale)
+    half = jnp.dot(
+        left,
+        jnp.concatenate([late_high, late_high, late_low], axis=0),
+        preferred_element_type=F32,
+    )
+    half_high, half_low = split(half)
+    half = jnp.concatenate([half_high, half_low, half_high], axis=1)
+    first = lax.dot_general(half, right, NT_DIMS, preferred_element_type=F32)
+    second = lax.dot_general(right, half, NT_DIMS, preferred_element_type=F32)
+    ritz_ref[...] = 0.5 * (base + (first + second))
 
     halo_sent(x_halo)
     halo_sent(p_halo)

time: 21.3 us -> 21.2 us (level)
  no operation moved by 1% of the time
where the time goes in v4:
time: 21.2 us; the launch traced here: 21.1 us
  Pallas kernels  18.4 us (87%)
  between operations  1.94 us (9%)
  local copies, waits for them, and re-layouts  0.75 us (4%)
    pallas_call x1, Pallas kernels, body(): pl.pallas_call(functools.partial(iterate_kernel, sizes, here * total), ou...  17.6 us
    concatenate x1, local copies, waits for them, and re-layouts, body(): jnp.concatenate([tile_cols, tile_rows, tile_count, locked, jnp.zeros((-us...  0.75 us
    pallas_call x1, Pallas kernels, body(): pl.pallas_call(store_kernel, out_shape=shapes, in_specs=[vmem] * 3, out_s...  0.73 us

profile of v4, /device:TPU:0, one launch (start us, length us, event | category | flops | bytes accessed | tf_op | source)
XLA Modules:
  0.0 21.1 jit_solution(17964154847379873690)
XLA Ops:
  1.9 0.8 %concatenate.3.ints_hbm = s32[128]{0:T(128)S(1)} concatenate(s32[48]{0:T(128)} %param.11, s32[48]{0:T(128)} %param.10, s32[1]{0:T(128)S(6)} %copy.10, s32[1]{0:T(128)S(6)} %copy.11, s32[30]{0:T(128)S(1)} %broadcast.3), dimensions={0} | concatenate | bytes 1024 | tf_op jit(solution)/shard_map/concatenate | solution.py:568
  2.7 17.6 %iterate.1 = (f32[16,2048]{1,0:T(8,128)S(1)}, f32[16,2048]{1,0:T(8,128)S(1)}, f32[48,48]{1,0:T(8,128)S(1)}) custom-call(s32[128]{0:T(128)S(1)} %concatenate.3.ints_hbm, f32[16,2048]{1,0:T(8,128)} %x_hbm.1, f32[16,2048]{1,0:T(8,128)} %p_hbm.1, f32[48,128,128]{2,1,0:T(8,128)} %tiles_hbm.1), custom_call_target="tpu_custom_call" | custom-call | tf_op jit(solution)/shard_map/iterate/pallas_call | solution.py:571
  20.3 0.7 %store.1 = (f32[16,2048]{1,0:T(8,128)}, f32[16,2048]{1,0:T(8,128)}, f32[48,48]{1,0:T(8,128)}) custom-call(f32[16,2048]{1,0:T(8,128)S(1)} %get-tuple-element.6.w_ref, f32[16,2048]{1,0:T(8,128)S(1)} %get-tuple-element.7.aw_ref, f32[48,48]{1,0:T(8,128)S(1)} %get-tuple-element.8.ritz_ref), custom_call_target="tpu_custom_call" | custom-call | tf_op jit(solution)/shard_map/store/pallas_call | solution.py:611
  (1 shorter events, 0.0 us)

commit v5 on v4

--- a/solution.py
+++ b/solution.py
@@ -59,9 +59,9 @@
 
 def iterate_kernel(
     sizes, vertex_total,
-    ints_hbm, x_hbm, p_hbm, tiles_hbm,
+    cols_in, rows_in, count_in, locked_in, x_hbm, p_hbm, tiles_hbm,
     w_ref, aw_ref, ritz_ref,
-    ints_ref, index_ref, before_ref, last_ref,
+    cols_ref, rows_ref, count_ref, locked_ref, index_ref, before_ref, last_ref,
     raw, halves, xh, ph, yh, q_buf, z_buf, seg, near_ref, far_ref, every, upper,
     int_sem, block_sem, tile_sem, halo_send, halo_recv, near_send, near_recv, far_send, far_recv,
     all_send, all_recv, relay,
@@ -168,8 +168,19 @@
         pltpu.make_async_copy(target.at[own], target.at[own], sem).wait()
 
     block_start(x_hbm, xh, block_sem.at[0])
-    int_copy = pltpu.make_async_copy(ints_hbm, ints_ref, int_sem.at[0])
-    int_copy.start()
+    int_copies = [
+        pltpu.make_async_copy(source, target, int_sem.at[i])
+        for i, (source, target) in enumerate(
+            (
+                (cols_in, cols_ref),
+                (rows_in, rows_ref),
+                (count_in, count_ref),
+                (locked_in, locked_ref),
+            )
+        )
+    ]
+    for copy in int_copies:
+        copy.start()
     tile_copies = []
     for c in range(chunks):
         part = pl.ds(c * chunk, chunk)
@@ -256,14 +267,15 @@
         lax.fori_loop(0, row_tiles // 8, step, 0)
 
     def tables():
-        int_copy.wait()
-        live = ints_ref[2 * slots]
+        for copy in int_copies:
+            copy.wait()
+        live = count_ref[0]
         base_col = position * row_tiles - reach
         base_row = position * row_tiles
         at = []
         for t in range(spare):
-            index_ref[t] = jnp.clip(ints_ref[row_tiles + t] - base_col, 0, 2 * row_tiles - 1)
-            row = jnp.where(row_tiles + t < live, ints_ref[slots + row_tiles + t] - base_row, -1)
+            index_ref[t] = jnp.clip(cols_ref[row_tiles + t] - base_col, 0, 2 * row_tiles - 1)
+            row = jnp.where(row_tiles + t < live, rows_ref[row_tiles + t] - base_row, -1)
             link = jnp.int32(0)
             for s in range(t):
                 link = jnp.where(at[s] == row, s + 1, link)
@@ -401,7 +413,7 @@
     all_z[0](pack(inner(basis, (parts(z_buf, 0),)), vectors))
 
     scale = 1.0 / vertex_total
-    locked = ints_ref[2 * slots + 1]
+    locked = locked_ref[0]
     by_xp = unpack(far_x[1](), 2 * vectors, 2 * vectors)
     by_y = unpack(all_y[1](), width, vectors)
     lane_w = iota((vectors, 128), 1)
@@ -564,17 +576,16 @@
         jax.ShapeDtypeStruct((vectors, here), F32),
         jax.ShapeDtypeStruct((width, width), F32),
     )
-    used = 2 * slots + 2
-    ints = jnp.concatenate(
-        [tile_cols, tile_rows, tile_count, locked, jnp.zeros((-used % 128,), jnp.int32)]
-    )
-    results = pl.pallas_call(
+    iterate = pl.pallas_call(
         functools.partial(iterate_kernel, sizes, here * total),
         out_shape=shapes,
-        in_specs=[anywhere] * 4,
+        in_specs=[anywhere] * 7,
         out_specs=(vmem, vmem, vmem),
         scratch_shapes=[
-            pltpu.SMEM(ints.shape, jnp.int32),
+            pltpu.SMEM((slots,), jnp.int32),
+            pltpu.SMEM((slots,), jnp.int32),
+            pltpu.SMEM((1,), jnp.int32),
+            pltpu.SMEM((1,), jnp.int32),
             pltpu.SMEM((spare,), jnp.int32),
             pltpu.SMEM((spare,), jnp.int32),
             pltpu.SMEM((row_tiles,), jnp.int32),
@@ -590,7 +601,7 @@
             pltpu.VMEM((4, row_count, EDGE, 128), F32),
             pltpu.VMEM((3, total, EDGE, 128), F32),
             pltpu.VMEM((width, 128), F32),
-            dma((1,)),
+            dma((4,)),
             dma((2,)),
             dma((slots // row_tiles,)),
             dma((3, 2)),
@@ -607,7 +618,13 @@
             collective_id=0, has_side_effects=True, vmem_limit_bytes=VMEM_ALL - VMEM_ROOM
         ),
         name="iterate",
-    )(ints, current_block, previous_block, adjacency_tiles)
+    )
+    results = lax.cond(
+        lax.axis_index("rows") >= 0,
+        iterate,
+        lambda *_: tuple(jnp.zeros(shape.shape, F32) for shape in shapes),
+        tile_cols, tile_rows, tile_count, locked, current_block, previous_block, adjacency_tiles,
+    )
     return pl.pallas_call(
         store_kernel,
         out_shape=shapes,

time: 21.2 us -> 20.6 us (0.972)
  Pallas kernels: 18.4 us -> 19.8 us
  between operations: 1.94 us -> 0.64 us
  local copies, waits for them, and re-layouts: 0.75 us -> 0 us
    pallas_call x1, Pallas kernels: 17.6 us -> 19.1 us  [body(): lax.cond(lax.axis_index('rows') >= 0, iterate, lambda *_: tuple((jnp.zero...]
    concatenate x1 -> x0, local copies, waits for them, and re-layouts: 0.75 us -> none  [body(): jnp.concatenate([tile_cols, tile_rows, tile_count, locked, jnp.zeros((-us...]
where the time goes in v5:
time: 20.6 us; the launch traced here: 20.5 us
  Pallas kernels  19.8 us (96%)
  between operations  0.64 us (3%)
    pallas_call x1, Pallas kernels, body(): lax.cond(lax.axis_index('rows') >= 0, iterate, lambda *_: tuple((jnp.zero...  19.1 us
    pallas_call x1, Pallas kernels, body(): pl.pallas_call(store_kernel, out_shape=shapes, in_specs=[vmem] * 3, out_s...  0.73 us

profile of v5, /device:TPU:0, one launch (start us, length us, event | category | flops | bytes accessed | tf_op | source)
XLA Modules:
  0.0 20.5 jit_solution(5781948458718780261)
XLA Ops:
  0.6 19.1 %conditional.1 = ((f32[16,2048]{1,0:T(8,128)S(1)}, f32[16,2048]{1,0:T(8,128)S(1)}, f32[48,48]{1,0:T(8,128)S(1)})) conditional(s32[]{:T(128)} %convert_element_type.3, () %tuple.14, (s32[48]{0:T(128)}, s32[48]{0:T(128)}, s32[1]{0:T(128)}, s32[1]{0:T(128)}, f32[16,2048]{1,0:T(8,128)}, /*index=5*/f32[16,2048]{1,0:T(8,128)}, ...), branch_computations={%region_0.0_spmd, %region_1.0_spmd} | conditional | bytes 271404 | solution.py:622
  0.6 19.1 %iterate.1 = (f32[16,2048]{1,0:T(8,128)S(1)}, f32[16,2048]{1,0:T(8,128)S(1)}, f32[48,48]{1,0:T(8,128)S(1)}) custom-call(s32[48]{0:T(128)} %get-tuple-element.37.cols_in, s32[48]{0:T(128)} %get-tuple-element.38.rows_in, s32[1]{0:T(128)} %get-tuple-element.39.count_in, s32[1]{0:T(128)} %get-tuple-element.40.locked_in, f32[16,2048]{1,0:T(8,128)} %get-tuple-element.41.x_hbm, ...), custom_call_target="tpu_custom_call" | custom-call | tf_op jit(solution)/shard_map/cond/branch_1_fun/iterate/pallas_call | solution.py:622
  19.7 0.7 %store.1 = (f32[16,2048]{1,0:T(8,128)}, f32[16,2048]{1,0:T(8,128)}, f32[48,48]{1,0:T(8,128)}) custom-call(f32[16,2048]{1,0:T(8,128)S(1)} %get-tuple-element.27.w_ref, f32[16,2048]{1,0:T(8,128)S(1)} %get-tuple-element.28.aw_ref, f32[48,48]{1,0:T(8,128)S(1)} %get-tuple-element.29.ritz_ref), custom_call_target="tpu_custom_call" | custom-call | tf_op jit(solution)/shard_map/store/pallas_call | solution.py:628

commit v6 on v5

--- a/solution.py
+++ b/solution.py
@@ -179,8 +179,6 @@
             )
         )
     ]
-    for copy in int_copies:
-        copy.start()
     tile_copies = []
     for c in range(chunks):
         part = pl.ds(c * chunk, chunk)
@@ -188,6 +186,8 @@
     tile_copies[0].start()
     block_start(p_hbm, ph, block_sem.at[1])
     for copy in tile_copies[1:]:
+        copy.start()
+    for copy in int_copies:
         copy.start()
 
     def halo_copies(buffer, which):
@@ -566,6 +566,7 @@
     total = row_count * near_count
     width = 3 * vectors
     spare = slots - row_tiles
+    stages = 1 if total <= 32 else 4
     vmem = pl.BlockSpec(memory_space=pltpu.VMEM)
     anywhere = pl.BlockSpec(memory_space=pl.ANY)
     dma = pltpu.SemaphoreType.DMA
@@ -597,8 +598,8 @@
             pltpu.VMEM(own, F32),
             pltpu.VMEM(own, F32),
             pltpu.VMEM((spare + 1, vectors, tile), F32),
-            pltpu.VMEM((4, near_count, EDGE, 128), F32),
-            pltpu.VMEM((4, row_count, EDGE, 128), F32),
+            pltpu.VMEM((stages, near_count, EDGE, 128), F32),
+            pltpu.VMEM((stages, row_count, EDGE, 128), F32),
             pltpu.VMEM((3, total, EDGE, 128), F32),
             pltpu.VMEM((width, 128), F32),
             dma((4,)),
@@ -606,10 +607,10 @@
             dma((slots // row_tiles,)),
             dma((3, 2)),
             dma((3, 2)),
-            dma((4,)),
-            dma((4,)),
-            dma((4,)),
-            dma((4,)),
+            dma((stages,)),
+            dma((stages,)),
+            dma((stages,)),
+            dma((stages,)),
             dma((3,)),
             dma((3,)),
             pltpu.SemaphoreType.REGULAR((2,)),

time: 20.6 us -> 20.5 us (level)
  no operation moved by 1% of the time
where the time goes in v6:
time: 20.5 us; the launch traced here: 20.4 us
  Pallas kernels  19.7 us (96%)
  between operations  0.64 us (3%)
    pallas_call x1, Pallas kernels, body(): lax.cond(lax.axis_index('rows') >= 0, iterate, lambda *_: tuple((jnp.zero...  19 us
    pallas_call x1, Pallas kernels, body(): pl.pallas_call(store_kernel, out_shape=shapes, in_specs=[vmem] * 3, out_s...  0.73 us

profile of v6, /device:TPU:0, one launch (start us, length us, event | category | flops | bytes accessed | tf_op | source)
XLA Modules:
  0.0 20.4 jit_solution(10457421511548465858)
XLA Ops:
  0.6 19.0 %conditional.1 = ((f32[16,2048]{1,0:T(8,128)S(1)}, f32[16,2048]{1,0:T(8,128)S(1)}, f32[48,48]{1,0:T(8,128)S(1)})) conditional(s32[]{:T(128)} %convert_element_type.3, () %tuple.14, (s32[48]{0:T(128)}, s32[48]{0:T(128)}, s32[1]{0:T(128)}, s32[1]{0:T(128)}, f32[16,2048]{1,0:T(8,128)}, /*index=5*/f32[16,2048]{1,0:T(8,128)}, ...), branch_computations={%region_0.0_spmd, %region_1.0_spmd} | conditional | bytes 271404 | solution.py:623
  0.6 19.0 %iterate.1 = (f32[16,2048]{1,0:T(8,128)S(1)}, f32[16,2048]{1,0:T(8,128)S(1)}, f32[48,48]{1,0:T(8,128)S(1)}) custom-call(s32[48]{0:T(128)} %get-tuple-element.37.cols_in, s32[48]{0:T(128)} %get-tuple-element.38.rows_in, s32[1]{0:T(128)} %get-tuple-element.39.count_in, s32[1]{0:T(128)} %get-tuple-element.40.locked_in, f32[16,2048]{1,0:T(8,128)} %get-tuple-element.41.x_hbm, ...), custom_call_target="tpu_custom_call" | custom-call | tf_op jit(solution)/shard_map/cond/branch_1_fun/iterate/pallas_call | solution.py:623
  19.6 0.7 %store.1 = (f32[16,2048]{1,0:T(8,128)}, f32[16,2048]{1,0:T(8,128)}, f32[48,48]{1,0:T(8,128)}) custom-call(f32[16,2048]{1,0:T(8,128)S(1)} %get-tuple-element.27.w_ref, f32[16,2048]{1,0:T(8,128)S(1)} %get-tuple-element.28.aw_ref, f32[48,48]{1,0:T(8,128)S(1)} %get-tuple-element.29.ritz_ref), custom_call_target="tpu_custom_call" | custom-call | tf_op jit(solution)/shard_map/store/pallas_call | solution.py:629
